TPU v7x, 32 devices: a whole 2x2x4 slice. The times are simulated.
32 devices in a mesh: groups: 2 (over y), expert: 4 (over z), mp: 4 (over x, core).
Axes of the slice: x: 2, y: 2, z: 4, core: 2. Of those that a mesh axis runs over, the one named last changes fastest.
Arguments:
- tokens: bfloat16 [6144, 1024], P(('groups', 'expert'), 'mp'), parts along dimension 0, may hold values from -60 to 60
- gain: float32 [1024], replicated, may hold values from 0.1 to 1.9
- w_res_in: bfloat16 [1024, 4096], P(None, 'mp'), may hold values from -0.1875 to 0.1875
- w_res_out: bfloat16 [4096, 1024], P('mp'), may hold values from -0.09375 to 0.09375
- w_exp_in: bfloat16 [4, 1024, 4096], P('expert', None, 'mp'), may hold values from -0.1875 to 0.1875
- w_exp_out: bfloat16 [4, 4096, 1024], P('expert', 'mp'), may hold values from -0.09375 to 0.09375
- expert_of: int32 [6144], P(('groups', 'expert')), parts along dimension 0, may hold values from 0 to 3
- slot_of: int32 [6144], P(('groups', 'expert')), parts along dimension 0, may hold values from -1 to 239, as said below
- gate_prob: float32 [6144], P(('groups', 'expert')), parts along dimension 0, may hold values from 0.2 to 1
Outputs:
- layer_out: bfloat16 [6144, 1024], P(('groups', 'expert'), 'mp'), parts along dimension 0
There are 2 independent parts, one for each index of `groups`. A program takes and returns all parts, laid end to end along the dimension named above; an argument that names none is the same for every part. Nothing has to cross between parts.
Inputs may be any that keep to these rules, and one draw needn't show every extreme that they name: slot_of[t] is the number of earlier tokens of t's aligned block of 768 tokens with the same expert_of, or -1 where that number is 240 or more. In every draw one expert has more than 240 tokens in every aligned block.
All inputs are finite; a program needn't handle non-finite values.
Results may differ from a plain program's by a relative error of at most 0.014.
Values may be sent and summed in bfloat16 or wider, within the bound.
A program may use at most 64 MiB of HBM per device.

v0:
```python
import jax
import jax.numpy as jnp
from jax import lax
from jax.sharding import PartitionSpec as P


def rms_rows(tokens, gain):
    values = tokens.astype(jnp.float32)
    inverse = lax.rsqrt(jnp.mean(values * values, axis=-1, keepdims=True) + 1e-05)
    return (values * inverse * gain).astype(jnp.bfloat16)


def per_device(
    tokens, gain, w_res_in, w_res_out, w_exp_in, w_exp_out, expert_of, slot_of, gate_prob
):
    full_rows = lax.all_gather(tokens, "mp", axis=1, tiled=True)
    normed = rms_rows(full_rows, gain)
    res_hidden = jax.nn.gelu(jnp.dot(normed, w_res_in, preferred_element_type=jnp.float32)).astype(
        jnp.bfloat16
    )
    res_part = jnp.dot(res_hidden, w_res_out, preferred_element_type=jnp.float32)
    row_count = expert_of.shape[0]
    experts = lax.axis_size("expert")
    capacity = max(2, 5 * row_count // (4 * experts))
    feat_width = tokens.shape[1]
    slot_id = jnp.where(slot_of >= 0, expert_of * capacity + slot_of, -1)
    slot_index = jnp.arange(experts * capacity, dtype=jnp.int32)
    send_table = (slot_index[:, None] == slot_id[None, :]).astype(jnp.bfloat16)
    take_table = (slot_id[:, None] == slot_index[None, :]).astype(jnp.bfloat16)
    local_in = w_exp_in[0]
    local_out = w_exp_out[0]
    mp_index = lax.axis_index("mp")
    own_slice = lax.dynamic_slice_in_dim(normed, mp_index * feat_width, feat_width, 1)
    outgoing = jnp.dot(send_table, own_slice, preferred_element_type=jnp.float32).astype(
        jnp.bfloat16
    )
    incoming = lax.all_to_all(
        outgoing.reshape(experts, capacity, feat_width),
        "expert",
        split_axis=0,
        concat_axis=0,
        tiled=True,
    )
    piece = lax.all_gather(incoming, "mp", axis=2, tiled=True)
    flat_piece = piece.reshape(-1, piece.shape[2])
    preact = jnp.dot(flat_piece, local_in, preferred_element_type=jnp.float32)
    exp_hidden = jax.nn.gelu(preact).astype(jnp.bfloat16)
    exp_part = jnp.dot(exp_hidden, local_out, preferred_element_type=jnp.float32)
    gate_column = gate_prob[:, None]
    summed = lax.psum_scatter(exp_part.astype(jnp.bfloat16), "mp", scatter_dimension=1, tiled=True)
    returned = lax.all_to_all(
        summed.reshape(experts, capacity, feat_width),
        "expert",
        split_axis=0,
        concat_axis=0,
        tiled=True,
    )
    moe_value = jnp.dot(
        take_table,
        returned.reshape(experts * capacity, feat_width),
        preferred_element_type=jnp.float32,
    )
    res_sum = lax.psum_scatter(
        res_part.astype(jnp.bfloat16), "mp", scatter_dimension=1, tiled=True
    ).astype(jnp.float32)
    return (res_sum + gate_column * moe_value).astype(jnp.bfloat16)


def solution(mesh):
    return jax.shard_map(
        per_device,
        mesh=mesh,
        in_specs=(
            P(("groups", "expert"), "mp"),
            P(),
            P(None, "mp"),
            P("mp", None),
            P("expert", None, "mp"),
            P("expert", "mp", None),
            P(("groups", "expert")),
            P(("groups", "expert")),
            P(("groups", "expert")),
        ),
        out_specs=P(("groups", "expert"), "mp"),
        check_vma=False,
    )
```

profile of v0, /device:TPU:0, one launch (start us, length us, event | category | flops | bytes accessed | tf_op | source)
XLA Modules:
  0.0 153.2 jit_solution(7485082166365213157)
XLA Ops:
  6.5 0.0 copy-start
  6.5 0.0 all-gather.3.cloned.1.call-start
  6.5 0.7 all-gather.3.cloned.1.call-update
  7.3 0.0 all-gather.5.cloned.1.call-start
  7.3 0.7 add_select_fusion
  8.0 23.4 %all-gather.3.cloned.1.call-done = bf16[768,1024]{1,0:T(8,128)(2,1)} async-done(((bf16[768,256]{1,0:T(8,128)(2,1)}), bf16[768,1024]{1,0:T(8,128)(2,1)}) %all-gather.3.cloned.1.call-update) | async-done | bytes 1572880 | tf_op jit(solution)/shard_map/all_gather | solution.py:16
  31.5 0.0 copy-start.1
  31.5 1.9 %fusion.8 = f32[768]{0:T(1024)S(1)} fusion(bf16[768,1024]{1,0:T(8,128)(2,1)} %all-gather.3.cloned.1.call-done), kind=kLoop, calls=%fused_computation.12 | loop fusion | flops 2358528 | bytes 1575936 | tf_op jit(solution)/shard_map/reduce_sum | solution.py:9
  33.4 0.0 copy-done.1
  33.4 1.1 fusion.10
  34.5 0.0 copy-start.2
  34.5 1.1 copy-done.2
  35.6 0.6 fusion.39
  36.3 18.7 %all_to_all.10 = bf16[4,240,256]{2,1,0:T(8,128)(2,1)} all-to-all(bf16[4,240,256]{2,1,0:T(8,128)(2,1)S(1)} %bitcast.23), channel_id=1, replica_groups=mesh['groups'=2,'expert'=4,'mp'=4] {'expert'}, dimensions={0} | all-to-all | bytes 983040 | tf_op jit(solution)/shard_map/all_to_all | solution.py:37
  55.0 0.0 all-gather.5.cloned.1.call-update
  55.0 0.0 reduce-scatter.5.cloned.1.call-start
  55.1 20.3 %all-gather.5.cloned.1.call-done = bf16[4,240,1024]{2,1,0:T(8,128)(2,1)} async-done(((bf16[4,240,256]{2,1,0:T(8,128)(2,1)}), bf16[4,240,1024]{2,1,0:T(8,128)(2,1)}) %all-gather.5.cloned.1.call-update) | async-done | bytes 1966096 | tf_op jit(solution)/shard_map/all_gather | solution.py:44
  75.4 0.0 copy-done
  75.4 7.8 %fusion.27 = bf16[960,1024]{1,0:T(8,128)(2,1)} fusion(bf16[1,1024,1024]{2,1,0:T(8,128)(2,1)S(1)} %copy-done, bf16[960,1024]{1,0:T(8,128)(2,1)} %bitcast.24, bf16[1,1024,1024]{2,1,0:T(8,128)(2,1)} %param.13), kind=kOutput, calls=%fused_computation.31 | convolution fusion | flops 4036362240 | bytes 8126464 | tf_op jit(solution)/shard_map/dot_general | solution.py:48
  83.2 0.0 reduce-scatter.5.cloned.1.call-update
  83.2 0.0 reduce-scatter.3.cloned.1.call-start
  83.2 7.4 %convolution_convert_fusion = bf16[768,1024]{1,0:T(8,128)(2,1)} fusion(bf16[1024,1024]{1,0:T(8,128)(2,1)} %param.12, bf16[768,1024]{1,0:T(8,128)(2,1)} %copy-done.2, bf16[1024,1024]{1,0:T(8,128)(2,1)} %param.11), kind=kOutput, calls=%fused_computation.32 | convolution fusion | flops 3229089792 | bytes 7340032 | tf_op jit(solution)/shard_map/dot_general | solution.py:21
  90.6 0.0 copy-start.3
  90.6 0.0 reduce-scatter.3.cloned.1.call-update
  90.6 23.1 %reduce-scatter.5.cloned.1.call-done = bf16[960,256]{1,0:T(8,128)(2,1)} async-done(((bf16[960,1024]{1,0:T(8,128)(2,1)}), bf16[960,256]{1,0:T(8,128)(2,1)}) %reduce-scatter.5.cloned.1.call-update) | async-done | bytes 491536 | tf_op jit(solution)/shard_map/reduce_scatter | solution.py:50
  113.7 4.6 %all-to-all-start.1 = ((bf16[4,240,256]{2,1,0:T(8,128)(2,1)}), bf16[4,240,256]{2,1,0:T(8,128)(2,1)S(1)}, u32[]{:S(2)}, u32[]{:S(2)}) async-start(bf16[4,240,256]{2,1,0:T(8,128)(2,1)} %bitcast.21), calls=%async_computation.3 | async-start | bytes 983040 | tf_op jit(solution)/shard_map/all_to_all | solution.py:51
  118.3 25.8 %reduce-scatter.3.cloned.1.call-done = bf16[768,256]{1,0:T(8,128)(2,1)} async-done(((bf16[768,1024]{1,0:T(8,128)(2,1)}), bf16[768,256]{1,0:T(8,128)(2,1)}) %reduce-scatter.3.cloned.1.call-update) | async-done | bytes 393232 | tf_op jit(solution)/shard_map/reduce_scatter | solution.py:63
  144.2 0.0 all-to-all-done.1
  144.2 0.0 copy-done.3
  144.2 2.5 %fusion.40 = bf16[768,256]{1,0:T(8,128)(2,1)} fusion(bf16[960,256]{1,0:T(8,128)(2,1)S(1)} %bitcast.22, s32[768]{0:T(1024)S(1)} %add_select_fusion, bf16[768,256]{1,0:T(8,128)(2,1)} %reduce-scatter.3.cloned.1.call-done, f32[768]{0:T(1024)S(1)} %copy-done.3), kind=kOutput, calls=%fused_computation.42 | convolution fusion | flops 379011072 | bytes 1284096 | tf_op jit(solution)/shard_map/dot_general | solution.py:58
  (1 shorter events, 0.0 us)
Async XLA Ops:
  6.5 68.9 %copy-start = (bf16[1,1024,1024]{2,1,0:T(8,128)(2,1)S(1)}, bf16[1,1024,1024]{2,1,0:T(8,128)(2,1)}, u32[]{:S(2)}) copy-start(bf16[1,1024,1024]{2,1,0:T(8,128)(2,1)} %param.14) | copy-start | bytes 6291460
  6.5 24.9 %all-gather.3.cloned.1.call-start = ((), (), s32[]{:S(2)}) async-start(), calls=%async_computation.4 | async-start | bytes 1966080 | tf_op jit(solution)/shard_map/all_gather | solution.py:16
  7.3 68.1 %all-gather.5.cloned.1.call-start = ((), (), s32[]{:S(2)}) async-start(), calls=%async_computation.6 | async-start | bytes 2457600 | tf_op jit(solution)/shard_map/all_gather | solution.py:44
  31.5 1.9 %copy-start.1 = (bf16[768,1024]{1,0:T(8,128)(2,1)S(1)}, bf16[768,1024]{1,0:T(8,128)(2,1)}, u32[]{:S(2)}) copy-start(bf16[768,1024]{1,0:T(8,128)(2,1)} %all-gather.3.cloned.1.call-done) | copy-start | bytes 4718596
  34.5 1.1 copy-start.2
  55.0 58.7 %reduce-scatter.5.cloned.1.call-start = ((), (), s32[]{:S(2)}) async-start(), calls=%async_computation.7 | async-start | bytes 2457600 | tf_op jit(solution)/shard_map/reduce_scatter | solution.py:50
  83.2 61.0 %reduce-scatter.3.cloned.1.call-start = ((), (), s32[]{:S(2)}) async-start(), calls=%async_computation.5 | async-start | bytes 1966080 | tf_op jit(solution)/shard_map/reduce_scatter | solution.py:63
  90.6 53.6 %copy-start.3 = (f32[768]{0:T(1024)S(1)}, f32[768]{0:T(1024)}, u32[]{:S(2)}) copy-start(f32[768]{0:T(1024)} %param.17) | copy-start | bytes 9220
  113.7 30.5 %all-to-all-start.1 = ((bf16[4,240,256]{2,1,0:T(8,128)(2,1)}), bf16[4,240,256]{2,1,0:T(8,128)(2,1)S(1)}, u32[]{:S(2)}, u32[]{:S(2)}) async-start(bf16[4,240,256]{2,1,0:T(8,128)(2,1)} %bitcast.21), calls=%async_computation.3 | async-start | bytes 983040 | tf_op jit(solution)/shard_map/all_to_all | solution.py:51
Sparse Core Ops, SparseCore 0:
  8.9 22.5 all-gather.2
  55.2 20.1 all-gather.4
  83.3 30.3 reduce-scatter.4
  116.1 28.0 reduce-scatter.2
where the time goes:
time: 154 us; the launch traced here: 153 us
  waiting for transfers between devices  93.4 us (61%)
  blocking collectives  18.7 us (12%)
  matrix products  18.3 us (12%)
  between operations  13.2 us (9%)
  starting transfers between devices  4.75 us (3%)
  other arithmetic  3.73 us (2%)
    reduce_scatter x1, waiting for transfers between devices, per_device(): lax.psum_scatter(res_part.astype(jnp.bfloat16), 'mp', scatter_dimension=1...  25.8 us
    all_gather x1, waiting for transfers between devices, per_device(): full_rows = lax.all_gather(tokens, 'mp', axis=1, tiled=True)  23.4 us
    reduce_scatter x1, waiting for transfers between devices, per_device(): lax.psum_scatter(exp_part.astype(jnp.bfloat16), 'mp', scatter_dimension=1...  23.1 us
    all_gather x1, waiting for transfers between devices, per_device(): piece = lax.all_gather(incoming, 'mp', axis=2, tiled=True)  20.3 us
    all_to_all x1, blocking collectives, per_device(): lax.all_to_all(outgoing.reshape(experts, capacity, feat_width), 'expert',...  18.7 us
    dot_general x1, matrix products, per_device(): jnp.dot(exp_hidden, local_out, preferred_element_type=jnp.float32)  7.77 us
    dot_general x1, matrix products, per_device(): jnp.dot(res_hidden, w_res_out, preferred_element_type=jnp.float32)  7.35 us
    all_to_all x1, starting transfers between devices, per_device(): lax.all_to_all(summed.reshape(experts, capacity, feat_width), 'expert', s...  4.62 us
  transfers between devices with their start and end apart: 5, of which 4 were waited for; matrix products, arithmetic and copies ran while one was open for 5% of the time, Pallas kernels for 0%

commit v1 on v0

--- a/solution.py
+++ b/solution.py
@@ -1,6 +1,8 @@
 import jax
 import jax.numpy as jnp
 from jax import lax
+from jax.experimental import pallas as pl
+from jax.experimental.pallas import tpu as pltpu
 from jax.sharding import PartitionSpec as P
 
 
@@ -66,9 +68,265 @@
     return (res_sum + gate_column * moe_value).astype(jnp.bfloat16)
 
 
+MESH = pl.DeviceIdType.MESH
+F32 = jnp.float32
+BF16 = jnp.bfloat16
+
+
+def dot(a, b):
+    return jnp.dot(a, b, preferred_element_type=F32)
+
+
+def first_layer(rows_ref, w_ref, hidden_ref, chunk):
+    def body(n, carry):
+        cols = pl.ds(pl.multiple_of(n * chunk, chunk), chunk)
+        hidden_ref[:, cols] = jax.nn.gelu(dot(rows_ref[...], w_ref[:, cols])).astype(BF16)
+        return carry
+
+    lax.fori_loop(0, hidden_ref.shape[1] // chunk, body, 0)
+
+
+def fused_kernel(
+    tokens, gain, w_ri_h, w_ro_h, w_ei_h, w_eo_h, expert_of, slot_of, gate_prob, out,
+    w_ri, w_ro, w_ei, w_eo, tok, normed, res_hid, rows_raw, out_rows, out_rows2, rows_near, rows_far,
+    hid, own_part, de_send, de_recv, e_keep, pair_send, pair_recv, xf_send, xf_recv, zf_send, zf_recv,
+    dt_send, dt_recv, t_keep, xt_send, xt_recv, gate_col, id_col, w_sem, send_sem, recv_sem,
+):
+    count, width = tokens.shape
+    cap = out_rows.shape[1]
+    shards = tok.shape[0]
+    me = lax.axis_index("mp")
+    z = lax.axis_index("expert")
+    core = lax.rem(me, 2)
+    over = lax.rem(me + 2, 4)
+    mate = me + 1 - 2 * core
+    cross = lax.rem(mate + 2, 4)
+    pair = z + 1 - 2 * lax.rem(z, 2)
+    far = (lax.rem(z + 2, 4), 3 - z)
+    to_over, to_mate, to_pair = {"mp": over}, {"mp": mate}, {"expert": pair}
+    to_far = ({"expert": far[0]}, {"expert": far[1]})
+
+    loads = []
+    for k, (src, dst) in enumerate(((w_ri_h, w_ri), (w_ei_h.at[0], w_ei), (w_eo_h.at[0], w_eo), (w_ro_h, w_ro))):
+        load = pltpu.make_async_copy(src, dst, w_sem.at[k])
+        load.start()
+        loads.append(load)
+
+    barrier = pltpu.get_barrier_semaphore()
+    for dest in (to_over, to_mate, to_pair, to_far[0], to_far[1]):
+        pl.semaphore_signal(barrier, inc=1, device_id=dest, device_id_type=MESH)
+
+    ids = jnp.where(slot_of[...] >= 0, expert_of[...] * cap + slot_of[...], -1).astype(F32)
+    slot_rows = lax.broadcasted_iota(jnp.int32, (cap, count), 0).astype(F32)
+    slot_cols = lax.broadcasted_iota(jnp.int32, (count, cap), 1).astype(F32)
+
+    def send_table(e):
+        base = (e * cap).astype(F32)
+        return jnp.where(slot_rows + base == ids, 1.0, 0.0).astype(BF16)
+
+    def take_table(e):
+        base = (e * cap).astype(F32)
+        return jnp.where(slot_cols + base == id_col[:, :1], 1.0, 0.0).astype(BF16)
+
+    sent = []
+
+    def send(src, dst, dest):
+        k = len(sent)
+        copy = pltpu.make_async_remote_copy(
+            src_ref=src, dst_ref=dst, send_sem=send_sem.at[k], recv_sem=recv_sem.at[k],
+            device_id=dest, device_id_type=MESH,
+        )
+        copy.start()
+        sent.append(copy)
+        return copy
+
+    pl.semaphore_wait(barrier, 5)
+    tok_over = send(tokens, tok.at[me], to_over)
+    tok_mate = send(tokens, tok.at[me], to_mate)
+    z_in = []
+    for f in range(2):
+        out_rows[f + 1] = dot(send_table(far[f]), tokens[...]).astype(BF16)
+        z_in.append(send(out_rows.at[f + 1], rows_raw.at[me, f + 1], to_far[f]))
+    pair_table = send_table(pair)
+    out_rows[0] = dot(pair_table, tokens[...]).astype(BF16)
+    pair_in = send(out_rows.at[0], rows_raw.at[me, 0], to_pair)
+    tok[me] = tokens[...]
+    id_col[...] = jnp.broadcast_to(ids, (128, count)).T
+    gate_col[...] = jnp.broadcast_to(gate_prob[...], (128, count)).T
+
+    tok_over.wait_recv()
+    tok_cross = send(tok.at[over], tok.at[over], to_mate)
+    out_rows2[...] = dot(pair_table, tok[over]).astype(BF16)
+    pair_in2 = send(out_rows2, rows_raw.at[over, 0], to_pair)
+    x_in, d_in = [], []
+    for f in range(2):
+        z_in[f].wait_recv()
+        piece = rows_raw.at[me, f + 1]
+        x_in.append(send(piece, piece, to_over))
+        d_in.append(send(piece, piece, to_mate))
+
+    def normalize(load, scale_rows, dst, lo):
+        total = 0.0
+        for s in range(shards):
+            v = load(s).astype(F32)
+            total = total + jnp.sum(v * v, axis=-1, keepdims=True)
+        inverse = lax.rsqrt(total / (shards * width) + 1e-05)
+        for s in range(shards):
+            cols = slice(s * width, (s + 1) * width)
+            dst[lo:lo + scale_rows, cols] = (load(s).astype(F32) * inverse * gain[:, cols]).astype(BF16)
+
+    tok_mate.wait_recv()
+    tok_cross.wait_recv()
+    normalize(lambda s: tok[s], count, normed, 0)
+    loads[0].wait()
+    first_layer(normed, w_ri, res_hid, width)
+
+    pair_in.wait_recv()
+    pair_d = send(rows_raw.at[me, 0], rows_raw.at[me, 0], to_mate)
+    pair_in2.wait_recv()
+    pair_d2 = send(rows_raw.at[over, 0], rows_raw.at[over, 0], to_mate)
+    rows_near[:cap, :] = dot(send_table(z), normed[...]).astype(BF16)
+    pair_d.wait_recv()
+    pair_d2.wait_recv()
+    normalize(lambda s: rows_raw[s, 0], cap, rows_near, cap)
+    loads[1].wait()
+    first_layer(rows_near, w_ei, hid, width)
+
+    d_in2 = []
+    for f in range(2):
+        x_in[f].wait_recv()
+        piece = rows_raw.at[over, f + 1]
+        d_in2.append(send(piece, piece, to_mate))
+
+    loads[2].wait()
+
+    def shard_cols(s):
+        return pl.ds(pl.multiple_of(s * width, width), width)
+
+    de = []
+    for j, s in enumerate((mate, cross)):
+        part = dot(hid[...], w_eo[:, shard_cols(s)])
+        own_part[s] = part[:cap].astype(BF16)
+        de_send[j, 0] = part[cap:].astype(BF16)
+        de.append(send(de_send.at[j, 0], de_recv.at[j, 0], to_mate))
+    for j, s in enumerate((me, over)):
+        part = dot(hid[...], w_eo[:, shard_cols(s)])
+        own_part[s] = part[:cap].astype(BF16)
+        e_keep[j, 0] = part[cap:]
+
+    pair_out = []
+    for j in range(2):
+        de[j].wait_recv()
+        pair_send[j] = (e_keep[j, 0] + de_recv[j, 0].astype(F32)).astype(BF16)
+        pair_out.append(send(pair_send.at[j], pair_recv.at[j], to_pair))
+
+    for f in range(2):
+        d_in[f].wait_recv()
+        d_in2[f].wait_recv()
+        normalize(lambda s, f=f: rows_raw[s, f + 1], cap, rows_far, f * cap)
+    first_layer(rows_far, w_ei, hid, width)
+    de_far = {}
+    for j, s in ((1, cross), (0, mate)):
+        part = dot(hid[...], w_eo[:, shard_cols(s)])
+        for f in range(2):
+            de_send[j, f + 1] = part[f * cap:(f + 1) * cap].astype(BF16)
+            de_far[j, f] = send(de_send.at[j, f + 1], de_recv.at[j, f + 1], to_mate)
+    for j, s in ((1, over), (0, me)):
+        part = dot(hid[...], w_eo[:, shard_cols(s)])
+        for f in range(2):
+            e_keep[j, f + 1] = part[f * cap:(f + 1) * cap]
+    xf = []
+    for f in range(2):
+        de_far[1, f].wait_recv()
+        xf_send[f] = (e_keep[1, f + 1] + de_recv[1, f + 1].astype(F32)).astype(BF16)
+        xf.append(send(xf_send.at[f], xf_recv.at[f], to_over))
+
+    loads[3].wait()
+    own_take = take_table(z)
+    dt = {}
+
+    def token_part(s):
+        return dot(res_hid[...], w_ro[:, shard_cols(s)]) + gate_col[:, :1] * dot(own_take, own_part[s])
+
+    for j, s in ((1, cross), (0, mate)):
+        dt_send[j] = token_part(s).astype(BF16)
+        dt[j] = send(dt_send.at[j], dt_recv.at[j], to_mate)
+    for j, s in ((1, over), (0, me)):
+        t_keep[j] = token_part(s)
+
+    pair_take = take_table(pair)
+
+    def chip_sum(j):
+        pair_out[j].wait_recv()
+        dt[j].wait_recv()
+        return t_keep[j] + dt_recv[j].astype(F32) + gate_col[:, :1] * dot(pair_take, pair_recv[j])
+
+    xt_send[...] = chip_sum(1).astype(BF16)
+    xt = send(xt_send, xt_recv, to_over)
+    zf = []
+    for f in range(2):
+        xf[f].wait_recv()
+        de_far[0, f].wait_recv()
+        full = e_keep[0, f + 1] + de_recv[0, f + 1].astype(F32) + xf_recv[f].astype(F32)
+        zf_send[f] = full.astype(BF16)
+        zf.append(send(zf_send.at[f], zf_recv.at[f], to_far[f]))
+    t_keep[0] = chip_sum(0)
+    for f in range(2):
+        zf[f].wait_recv()
+        t_keep[0] = t_keep[0] + gate_col[:, :1] * dot(take_table(far[f]), zf_recv[f])
+    xt.wait_recv()
+    out[...] = (t_keep[0] + xt_recv[...].astype(F32)).astype(BF16)
+    for copy in sent:
+        copy.wait_send()
+
+
+def fused(tokens, gain, w_res_in, w_res_out, w_exp_in, w_exp_out, expert_of, slot_of, gate_prob):
+    count, width = tokens.shape
+    shards = lax.axis_size("mp")
+    experts = lax.axis_size("expert")
+    cap = max(2, 5 * count // (4 * experts))
+    model, hidden = w_res_in.shape
+    exp_hidden = w_exp_in.shape[2]
+    vmem, hbm = pl.BlockSpec(memory_space=pltpu.VMEM), pl.BlockSpec(memory_space=pl.ANY)
+    buf = lambda *shape: pltpu.VMEM(shape, BF16)
+    wide = lambda *shape: pltpu.VMEM(shape, F32)
+    copies = 30
+    return pl.pallas_call(
+        fused_kernel,
+        out_shape=jax.ShapeDtypeStruct((count, width), BF16),
+        in_specs=[vmem, vmem, hbm, hbm, hbm, hbm, vmem, vmem, vmem],
+        out_specs=vmem,
+        scratch_shapes=[
+            buf(model, hidden), buf(hidden, model), buf(model, exp_hidden), buf(exp_hidden, model),
+            buf(shards, count, width), buf(count, model), buf(count, hidden),
+            buf(shards, 3, cap, width), buf(3, cap, width), buf(cap, width),
+            buf(2 * cap, model), buf(2 * cap, model), buf(2 * cap, exp_hidden),
+            buf(shards, cap, width), buf(2, 3, cap, width), buf(2, 3, cap, width), wide(2, 3, cap, width),
+            buf(2, cap, width), buf(2, cap, width), buf(2, cap, width), buf(2, cap, width),
+            buf(2, cap, width), buf(2, cap, width),
+            buf(2, count, width), buf(2, count, width), wide(2, count, width),
+            buf(count, width), buf(count, width), wide(count, 128), wide(count, 128),
+            pltpu.SemaphoreType.DMA((4,)), pltpu.SemaphoreType.DMA((copies,)), pltpu.SemaphoreType.DMA((copies,)),
+        ],
+        name="fused_layer",
+        compiler_params=pltpu.CompilerParams(
+            collective_id=0, has_side_effects=True, vmem_limit_bytes=56 * 1024 * 1024
+        ),
+    )(
+        tokens, gain[None, :], w_res_in, w_res_out, w_exp_in, w_exp_out,
+        expert_of[None, :], slot_of[None, :], gate_prob[None, :],
+    )
+
+
+def pick(mesh):
+    if mesh.shape["mp"] == 4 and mesh.shape["expert"] == 4:
+        return fused
+    return per_device
+
+
 def solution(mesh):
     return jax.shard_map(
-        per_device,
+        pick(mesh),
         mesh=mesh,
         in_specs=(
             P(("groups", "expert"), "mp"),

time: 154 us -> 54.7 us (0.36)
  waiting for transfers between devices: 93.4 us -> 0 us
  Pallas kernels: 0 us -> 48.8 us
  blocking collectives: 18.7 us -> 0 us
  matrix products: 18.3 us -> 0 us
  between operations: 13.2 us -> 0.01 us
  starting transfers between devices: 4.75 us -> 0 us
  local copies, waits for them, and re-layouts: 1.15 us -> 5.57 us
  other arithmetic: 3.73 us -> 0 us
    reduce_scatter x2 -> x0, waiting for transfers between devices: 49 us -> none  [the longest x1 25.8 us: per_device(): lax.psum_scatter(res_part.astype(jnp.bfloat16), 'mp', scatter_dimension=1...]
    pallas_call x0 -> x1, Pallas kernels: none -> 48.8 us  [fused(): pl.pallas_call(fused_kernel, out_shape=jax.ShapeDtypeStruct((count, width...]
    all_gather x2 -> x0, waiting for transfers between devices: 43.7 us -> none  [the longest x1 23.4 us: per_device(): full_rows = lax.all_gather(tokens, 'mp', axis=1, tiled=True)]
    all_to_all x1 -> x0, blocking collectives: 18.7 us -> none  [per_device(): lax.all_to_all(outgoing.reshape(experts, capacity, feat_width), 'expert',...]
    dot_general x4 -> x0, matrix products: 18.3 us -> none  [the longest x1 7.77 us: per_device(): jnp.dot(exp_hidden, local_out, preferred_element_type=jnp.float32)]
    all_to_all x1 -> x0, starting transfers between devices: 4.62 us -> none  [per_device(): lax.all_to_all(summed.reshape(experts, capacity, feat_width), 'expert', s...]
    broadcast_in_dim x0 -> x3, local copies, waits for them, and re-layouts: none -> 3.81 us  [the longest x1 1.28 us: fused(): gate_prob[None, :]]
    reduce_sum x1 -> x0, other arithmetic: 1.9 us -> none  [rms_rows(): jnp.mean(values * values, axis=-1, keepdims=True) + 1e-05]
  transfers between devices with their start and end apart: 5 -> 0, of which waited for: 4 -> 0; matrix products, arithmetic and copies ran while one was open for 5% -> 0% of each run, Pallas kernels for 0% -> 0%
where the time goes in v1:
time: 54.7 us; the launch traced here: 54.4 us
  Pallas kernels  48.8 us (89%)
  local copies, waits for them, and re-layouts  5.57 us (10%)
    pallas_call x1, Pallas kernels, fused(): pl.pallas_call(fused_kernel, out_shape=jax.ShapeDtypeStruct((count, width...  48.8 us
    unnamed x1, local copies, waits for them, and re-layouts  1.77 us
    broadcast_in_dim x1, local copies, waits for them, and re-layouts, fused(): gate_prob[None, :]  1.28 us
    broadcast_in_dim x1, local copies, waits for them, and re-layouts, fused(): expert_of[None, :]  1.27 us
    broadcast_in_dim x1, local copies, waits for them, and re-layouts, fused(): slot_of[None, :]  1.27 us

profile of v1, /device:TPU:0, one launch (start us, length us, event | category | flops | bytes accessed | tf_op | source)
XLA Modules:
  0.0 54.4 jit_solution(13844281198101678379)
XLA Ops:
  0.0 1.3 %broadcast_in_dim.13.expert_of = s32[1,768]{1,0:T(1,128)} reshape(s32[768]{0:T(1024)} %param.15) | data formatting | bytes 6144 | tf_op jit(solution)/shard_map/broadcast_in_dim | solution.py:317
  1.3 1.3 %broadcast_in_dim.14.slot_of = s32[1,768]{1,0:T(1,128)} reshape(s32[768]{0:T(1024)} %param.16) | data formatting | bytes 6144 | tf_op jit(solution)/shard_map/broadcast_in_dim | solution.py:317
  2.5 1.3 %broadcast_in_dim.15.gate_prob = f32[1,768]{1,0:T(1,128)} reshape(f32[768]{0:T(1024)} %param.17) | data formatting | bytes 6144 | tf_op jit(solution)/shard_map/broadcast_in_dim | solution.py:317
  3.8 48.8 %fused_layer.1 = bf16[768,256]{1,0:T(8,128)(2,1)} custom-call(bf16[768,256]{1,0:T(8,128)(2,1)} %tokens.1, f32[1,1024]{1,0:T(1,128)} %bitcast.1, bf16[1024,1024]{1,0:T(8,128)(2,1)} %w_ri_h.1, bf16[1024,1024]{1,0:T(8,128)(2,1)} %w_ro_h.1, bf16[1,1024,1024]{2,1,0:T(8,128)(2,1)} %w_ei_h.1, bf16[1,1024,1024]{2,1,0:T(8,128)(2,1)} %w_eo_h.1, ...), custom_call_target="tpu_custom_call" | custom-call | tf_op jit(solution)/shard_map/fused_layer/pallas_call | solution.py:294
  52.6 1.8 %copy.11 = bf16[768,256]{1,0:T(8,128)(2,1)} copy(bf16[768,256]{1,0:T(8,128)(2,1)} %fused_layer.1) | data formatting | bytes 786432

commit v2 on v1

--- a/solution.py
+++ b/solution.py
@@ -1,3 +1,5 @@
+import functools
+
 import jax
 import jax.numpy as jnp
 from jax import lax
@@ -77,19 +79,19 @@
     return jnp.dot(a, b, preferred_element_type=F32)
 
 
-def first_layer(rows_ref, w_ref, hidden_ref, chunk):
+def first_layer(rows_ref, w_ref, hidden_ref, chunk, lo, size):
     def body(n, carry):
         cols = pl.ds(pl.multiple_of(n * chunk, chunk), chunk)
-        hidden_ref[:, cols] = jax.nn.gelu(dot(rows_ref[...], w_ref[:, cols])).astype(BF16)
+        hidden_ref[lo:lo + size, cols] = jax.nn.gelu(dot(rows_ref[lo:lo + size], w_ref[:, cols])).astype(BF16)
         return carry
 
     lax.fori_loop(0, hidden_ref.shape[1] // chunk, body, 0)
 
 
 def fused_kernel(
-    tokens, gain, w_ri_h, w_ro_h, w_ei_h, w_eo_h, expert_of, slot_of, gate_prob, out,
+    halves, tokens, gain, w_ri_h, w_ro_h, w_ei_h, w_eo_h, expert_of, slot_of, gate_prob, out,
     w_ri, w_ro, w_ei, w_eo, tok, normed, res_hid, rows_raw, out_rows, out_rows2, rows_near, rows_far,
-    hid, own_part, de_send, de_recv, e_keep, pair_send, pair_recv, xf_send, xf_recv, zf_send, zf_recv,
+    hid_near, hid, own_part, de_send, de_recv, e_keep, pair_send, pair_recv, xf_send, xf_recv, zf_send, zf_recv,
     dt_send, dt_recv, t_keep, xt_send, xt_recv, gate_col, id_col, w_sem, send_sem, recv_sem,
 ):
     count, width = tokens.shape
@@ -141,7 +143,9 @@
         return copy
 
     pl.semaphore_wait(barrier, 5)
-    tok_over = send(tokens, tok.at[me], to_over)
+    half = count // halves
+    spans = [slice(h * half, (h + 1) * half) for h in range(halves)]
+    tok_over = [send(tokens.at[r], tok.at[me, r], to_over) for r in spans]
     tok_mate = send(tokens, tok.at[me], to_mate)
     z_in = []
     for f in range(2):
@@ -153,17 +157,6 @@
     tok[me] = tokens[...]
     id_col[...] = jnp.broadcast_to(ids, (128, count)).T
     gate_col[...] = jnp.broadcast_to(gate_prob[...], (128, count)).T
-
-    tok_over.wait_recv()
-    tok_cross = send(tok.at[over], tok.at[over], to_mate)
-    out_rows2[...] = dot(pair_table, tok[over]).astype(BF16)
-    pair_in2 = send(out_rows2, rows_raw.at[over, 0], to_pair)
-    x_in, d_in = [], []
-    for f in range(2):
-        z_in[f].wait_recv()
-        piece = rows_raw.at[me, f + 1]
-        x_in.append(send(piece, piece, to_over))
-        d_in.append(send(piece, piece, to_mate))
 
     def normalize(load, scale_rows, dst, lo):
         total = 0.0
@@ -175,11 +168,38 @@
             cols = slice(s * width, (s + 1) * width)
             dst[lo:lo + scale_rows, cols] = (load(s).astype(F32) * inverse * gain[:, cols]).astype(BF16)
 
+
+    def shard_cols(s):
+        return pl.ds(pl.multiple_of(s * width, width), width)
+
+    tok_cross = []
+
+    def relay(h):
+        tok_over[h].wait_recv()
+        piece = tok.at[over, spans[h]]
+        tok_cross.append(send(piece, piece, to_mate))
+
+    def residual(h):
+        r = spans[h]
+        tok_cross[h].wait_recv()
+        normalize(lambda s: tok[s, r], half, normed, h * half)
+        first_layer(normed, w_ri, res_hid, width, h * half, half)
+
+    relay(0)
     tok_mate.wait_recv()
-    tok_cross.wait_recv()
-    normalize(lambda s: tok[s], count, normed, 0)
     loads[0].wait()
-    first_layer(normed, w_ri, res_hid, width)
+    for h in range(halves - 1):
+        residual(h)
+        relay(h + 1)
+    out_rows2[...] = dot(pair_table, tok[over]).astype(BF16)
+    pair_in2 = send(out_rows2, rows_raw.at[over, 0], to_pair)
+    x_in, d_in = [], []
+    for f in range(2):
+        z_in[f].wait_recv()
+        piece = rows_raw.at[me, f + 1]
+        x_in.append(send(piece, piece, to_over))
+        d_in.append(send(piece, piece, to_mate))
+    residual(halves - 1)
 
     pair_in.wait_recv()
     pair_d = send(rows_raw.at[me, 0], rows_raw.at[me, 0], to_mate)
@@ -190,90 +210,96 @@
     pair_d2.wait_recv()
     normalize(lambda s: rows_raw[s, 0], cap, rows_near, cap)
     loads[1].wait()
-    first_layer(rows_near, w_ei, hid, width)
+    first_layer(rows_near, w_ei, hid_near, width, 0, 2 * cap)
 
     d_in2 = []
     for f in range(2):
         x_in[f].wait_recv()
         piece = rows_raw.at[over, f + 1]
         d_in2.append(send(piece, piece, to_mate))
-
     loads[2].wait()
-
-    def shard_cols(s):
-        return pl.ds(pl.multiple_of(s * width, width), width)
-
-    de = []
-    for j, s in enumerate((mate, cross)):
-        part = dot(hid[...], w_eo[:, shard_cols(s)])
-        own_part[s] = part[:cap].astype(BF16)
-        de_send[j, 0] = part[cap:].astype(BF16)
-        de.append(send(de_send.at[j, 0], de_recv.at[j, 0], to_mate))
-    for j, s in enumerate((me, over)):
-        part = dot(hid[...], w_eo[:, shard_cols(s)])
-        own_part[s] = part[:cap].astype(BF16)
-        e_keep[j, 0] = part[cap:]
-
-    pair_out = []
-    for j in range(2):
-        de[j].wait_recv()
-        pair_send[j] = (e_keep[j, 0] + de_recv[j, 0].astype(F32)).astype(BF16)
-        pair_out.append(send(pair_send.at[j], pair_recv.at[j], to_pair))
-
     for f in range(2):
         d_in[f].wait_recv()
         d_in2[f].wait_recv()
         normalize(lambda s, f=f: rows_raw[s, f + 1], cap, rows_far, f * cap)
-    first_layer(rows_far, w_ei, hid, width)
-    de_far = {}
-    for j, s in ((1, cross), (0, mate)):
+    first_layer(rows_far, w_ei, hid, width, 0, 2 * cap)
+    de_far, xf = {}, []
+
+    def far_give(j, s):
         part = dot(hid[...], w_eo[:, shard_cols(s)])
         for f in range(2):
             de_send[j, f + 1] = part[f * cap:(f + 1) * cap].astype(BF16)
             de_far[j, f] = send(de_send.at[j, f + 1], de_recv.at[j, f + 1], to_mate)
-    for j, s in ((1, over), (0, me)):
+
+    def far_keep(j, s):
         part = dot(hid[...], w_eo[:, shard_cols(s)])
         for f in range(2):
             e_keep[j, f + 1] = part[f * cap:(f + 1) * cap]
-    xf = []
+
+    far_give(1, cross)
+    far_keep(1, over)
+    far_give(0, mate)
     for f in range(2):
         de_far[1, f].wait_recv()
         xf_send[f] = (e_keep[1, f + 1] + de_recv[1, f + 1].astype(F32)).astype(BF16)
         xf.append(send(xf_send.at[f], xf_recv.at[f], to_over))
+    far_keep(0, me)
+
+    de = {}
+    for j, s in ((1, cross), (0, mate)):
+        part = dot(hid_near[...], w_eo[:, shard_cols(s)])
+        own_part[s] = part[:cap].astype(BF16)
+        de_send[j, 0] = part[cap:].astype(BF16)
+        de[j] = send(de_send.at[j, 0], de_recv.at[j, 0], to_mate)
+    for j, s in ((1, over), (0, me)):
+        part = dot(hid_near[...], w_eo[:, shard_cols(s)])
+        own_part[s] = part[:cap].astype(BF16)
+        e_keep[j, 0] = part[cap:]
+    pair_out = {}
+    for j in (1, 0):
+        de[j].wait_recv()
+        pair_send[j] = (e_keep[j, 0] + de_recv[j, 0].astype(F32)).astype(BF16)
+        pair_out[j] = send(pair_send.at[j], pair_recv.at[j], to_pair)
 
     loads[3].wait()
     own_take = take_table(z)
+    pair_take = take_table(pair)
     dt = {}
 
     def token_part(s):
         return dot(res_hid[...], w_ro[:, shard_cols(s)]) + gate_col[:, :1] * dot(own_take, own_part[s])
 
-    for j, s in ((1, cross), (0, mate)):
+    def token_give(j, s):
         dt_send[j] = token_part(s).astype(BF16)
         dt[j] = send(dt_send.at[j], dt_recv.at[j], to_mate)
-    for j, s in ((1, over), (0, me)):
-        t_keep[j] = token_part(s)
-
-    pair_take = take_table(pair)
 
     def chip_sum(j):
         pair_out[j].wait_recv()
         dt[j].wait_recv()
         return t_keep[j] + dt_recv[j].astype(F32) + gate_col[:, :1] * dot(pair_take, pair_recv[j])
 
-    xt_send[...] = chip_sum(1).astype(BF16)
-    xt = send(xt_send, xt_recv, to_over)
     zf = []
-    for f in range(2):
+
+    def far_home(f):
         xf[f].wait_recv()
         de_far[0, f].wait_recv()
         full = e_keep[0, f + 1] + de_recv[0, f + 1].astype(F32) + xf_recv[f].astype(F32)
         zf_send[f] = full.astype(BF16)
         zf.append(send(zf_send.at[f], zf_recv.at[f], to_far[f]))
+
+    token_give(1, cross)
+    t_keep[1] = token_part(over)
+    far_home(0)
+    xt_send[...] = chip_sum(1).astype(BF16)
+    xt = send(xt_send, xt_recv, to_over)
+    far_home(1)
+    token_give(0, mate)
+    t_keep[0] = token_part(me)
     t_keep[0] = chip_sum(0)
     for f in range(2):
+        far_take = take_table(far[f])
         zf[f].wait_recv()
-        t_keep[0] = t_keep[0] + gate_col[:, :1] * dot(take_table(far[f]), zf_recv[f])
+        t_keep[0] = t_keep[0] + gate_col[:, :1] * dot(far_take, zf_recv[f])
     xt.wait_recv()
     out[...] = (t_keep[0] + xt_recv[...].astype(F32)).astype(BF16)
     for copy in sent:
@@ -290,9 +316,10 @@
     vmem, hbm = pl.BlockSpec(memory_space=pltpu.VMEM), pl.BlockSpec(memory_space=pl.ANY)
     buf = lambda *shape: pltpu.VMEM(shape, BF16)
     wide = lambda *shape: pltpu.VMEM(shape, F32)
-    copies = 30
+    halves = 2
+    copies = 28 + 2 * halves
     return pl.pallas_call(
-        fused_kernel,
+        functools.partial(fused_kernel, halves),
         out_shape=jax.ShapeDtypeStruct((count, width), BF16),
         in_specs=[vmem, vmem, hbm, hbm, hbm, hbm, vmem, vmem, vmem],
         out_specs=vmem,
@@ -300,7 +327,7 @@
             buf(model, hidden), buf(hidden, model), buf(model, exp_hidden), buf(exp_hidden, model),
             buf(shards, count, width), buf(count, model), buf(count, hidden),
             buf(shards, 3, cap, width), buf(3, cap, width), buf(cap, width),
-            buf(2 * cap, model), buf(2 * cap, model), buf(2 * cap, exp_hidden),
+            buf(2 * cap, model), buf(2 * cap, model), buf(2 * cap, exp_hidden), buf(2 * cap, exp_hidden),
             buf(shards, cap, width), buf(2, 3, cap, width), buf(2, 3, cap, width), wide(2, 3, cap, width),
             buf(2, cap, width), buf(2, cap, width), buf(2, cap, width), buf(2, cap, width),
             buf(2, cap, width), buf(2, cap, width),

time: 54.7 us -> 57.1 us (1.044)
  Pallas kernels: 48.8 us -> 51.2 us
    pallas_call x1, Pallas kernels: 48.8 us -> 51.2 us  [fused(): pl.pallas_call(functools.partial(fused_kernel, halves), out_shape=jax.Sha...]
where the time goes in v2:
time: 57.1 us; the launch traced here: 56.8 us
  Pallas kernels  51.2 us (90%)
  local copies, waits for them, and re-layouts  5.57 us (10%)
    pallas_call x1, Pallas kernels, fused(): pl.pallas_call(functools.partial(fused_kernel, halves), out_shape=jax.Sha...  51.2 us
    unnamed x1, local copies, waits for them, and re-layouts  1.77 us
    broadcast_in_dim x1, local copies, waits for them, and re-layouts, fused(): gate_prob[None, :]  1.28 us
    broadcast_in_dim x1, local copies, waits for them, and re-layouts, fused(): expert_of[None, :]  1.27 us
    broadcast_in_dim x1, local copies, waits for them, and re-layouts, fused(): slot_of[None, :]  1.27 us

profile of v2, /device:TPU:0, one launch (start us, length us, event | category | flops | bytes accessed | tf_op | source)
XLA Modules:
  0.0 56.8 jit_solution(15316771422542565660)
XLA Ops:
  0.0 1.3 %broadcast_in_dim.13.expert_of = s32[1,768]{1,0:T(1,128)} reshape(s32[768]{0:T(1024)} %param.15) | data formatting | bytes 6144 | tf_op jit(solution)/shard_map/broadcast_in_dim | solution.py:344
  1.3 1.3 %broadcast_in_dim.14.slot_of = s32[1,768]{1,0:T(1,128)} reshape(s32[768]{0:T(1024)} %param.16) | data formatting | bytes 6144 | tf_op jit(solution)/shard_map/broadcast_in_dim | solution.py:344
  2.5 1.3 %broadcast_in_dim.15.gate_prob = f32[1,768]{1,0:T(1,128)} reshape(f32[768]{0:T(1024)} %param.17) | data formatting | bytes 6144 | tf_op jit(solution)/shard_map/broadcast_in_dim | solution.py:344
  3.8 51.2 %fused_layer.1 = bf16[768,256]{1,0:T(8,128)(2,1)} custom-call(bf16[768,256]{1,0:T(8,128)(2,1)} %tokens.1, f32[1,1024]{1,0:T(1,128)} %bitcast.1, bf16[1024,1024]{1,0:T(8,128)(2,1)} %w_ri_h.1, bf16[1024,1024]{1,0:T(8,128)(2,1)} %w_ro_h.1, bf16[1,1024,1024]{2,1,0:T(8,128)(2,1)} %w_ei_h.1, bf16[1,1024,1024]{2,1,0:T(8,128)(2,1)} %w_eo_h.1, ...), custom_call_target="tpu_custom_call" | custom-call | tf_op jit(solution)/shard_map/fused_layer/pallas_call | solution.py:321
  55.0 1.8 %copy.11 = bf16[768,256]{1,0:T(8,128)(2,1)} copy(bf16[768,256]{1,0:T(8,128)(2,1)} %fused_layer.1) | data formatting | bytes 786432

commit v3 on v2

--- a/solution.py
+++ b/solution.py
@@ -218,33 +218,6 @@
         piece = rows_raw.at[over, f + 1]
         d_in2.append(send(piece, piece, to_mate))
     loads[2].wait()
-    for f in range(2):
-        d_in[f].wait_recv()
-        d_in2[f].wait_recv()
-        normalize(lambda s, f=f: rows_raw[s, f + 1], cap, rows_far, f * cap)
-    first_layer(rows_far, w_ei, hid, width, 0, 2 * cap)
-    de_far, xf = {}, []
-
-    def far_give(j, s):
-        part = dot(hid[...], w_eo[:, shard_cols(s)])
-        for f in range(2):
-            de_send[j, f + 1] = part[f * cap:(f + 1) * cap].astype(BF16)
-            de_far[j, f] = send(de_send.at[j, f + 1], de_recv.at[j, f + 1], to_mate)
-
-    def far_keep(j, s):
-        part = dot(hid[...], w_eo[:, shard_cols(s)])
-        for f in range(2):
-            e_keep[j, f + 1] = part[f * cap:(f + 1) * cap]
-
-    far_give(1, cross)
-    far_keep(1, over)
-    far_give(0, mate)
-    for f in range(2):
-        de_far[1, f].wait_recv()
-        xf_send[f] = (e_keep[1, f + 1] + de_recv[1, f + 1].astype(F32)).astype(BF16)
-        xf.append(send(xf_send.at[f], xf_recv.at[f], to_over))
-    far_keep(0, me)
-
     de = {}
     for j, s in ((1, cross), (0, mate)):
         part = dot(hid_near[...], w_eo[:, shard_cols(s)])
@@ -260,6 +233,33 @@
         de[j].wait_recv()
         pair_send[j] = (e_keep[j, 0] + de_recv[j, 0].astype(F32)).astype(BF16)
         pair_out[j] = send(pair_send.at[j], pair_recv.at[j], to_pair)
+
+    for f in range(2):
+        d_in[f].wait_recv()
+        d_in2[f].wait_recv()
+        normalize(lambda s, f=f: rows_raw[s, f + 1], cap, rows_far, f * cap)
+    first_layer(rows_far, w_ei, hid, width, 0, 2 * cap)
+    de_far, xf = {}, []
+
+    def far_give(j, s):
+        part = dot(hid[...], w_eo[:, shard_cols(s)])
+        for f in range(2):
+            de_send[j, f + 1] = part[f * cap:(f + 1) * cap].astype(BF16)
+            de_far[j, f] = send(de_send.at[j, f + 1], de_recv.at[j, f + 1], to_mate)
+
+    def far_keep(j, s):
+        part = dot(hid[...], w_eo[:, shard_cols(s)])
+        for f in range(2):
+            e_keep[j, f + 1] = part[f * cap:(f + 1) * cap]
+
+    far_give(1, cross)
+    far_keep(1, over)
+    far_give(0, mate)
+    for f in range(2):
+        de_far[1, f].wait_recv()
+        xf_send[f] = (e_keep[1, f + 1] + de_recv[1, f + 1].astype(F32)).astype(BF16)
+        xf.append(send(xf_send.at[f], xf_recv.at[f], to_over))
+    far_keep(0, me)
 
     loads[3].wait()
     own_take = take_table(z)

time: 57.1 us -> 54 us (0.946)
  Pallas kernels: 51.2 us -> 48.1 us
    pallas_call x1, Pallas kernels: 51.2 us -> 48.1 us  [fused(): pl.pallas_call(functools.partial(fused_kernel, halves), out_shape=jax.Sha...]
where the time goes in v3:
time: 54 us; the launch traced here: 53.7 us
  Pallas kernels  48.1 us (89%)
  local copies, waits for them, and re-layouts  5.57 us (10%)
    pallas_call x1, Pallas kernels, fused(): pl.pallas_call(functools.partial(fused_kernel, halves), out_shape=jax.Sha...  48.1 us
    unnamed x1, local copies, waits for them, and re-layouts  1.77 us
    broadcast_in_dim x1, local copies, waits for them, and re-layouts, fused(): gate_prob[None, :]  1.28 us
    broadcast_in_dim x1, local copies, waits for them, and re-layouts, fused(): expert_of[None, :]  1.27 us
    broadcast_in_dim x1, local copies, waits for them, and re-layouts, fused(): slot_of[None, :]  1.27 us

profile of v3, /device:TPU:0, one launch (start us, length us, event | category | flops | bytes accessed | tf_op | source)
XLA Modules:
  0.0 53.7 jit_solution(5149694623706680710)
XLA Ops:
  0.0 1.3 %broadcast_in_dim.13.expert_of = s32[1,768]{1,0:T(1,128)} reshape(s32[768]{0:T(1024)} %param.15) | data formatting | bytes 6144 | tf_op jit(solution)/shard_map/broadcast_in_dim | solution.py:344
  1.3 1.3 %broadcast_in_dim.14.slot_of = s32[1,768]{1,0:T(1,128)} reshape(s32[768]{0:T(1024)} %param.16) | data formatting | bytes 6144 | tf_op jit(solution)/shard_map/broadcast_in_dim | solution.py:344
  2.5 1.3 %broadcast_in_dim.15.gate_prob = f32[1,768]{1,0:T(1,128)} reshape(f32[768]{0:T(1024)} %param.17) | data formatting | bytes 6144 | tf_op jit(solution)/shard_map/broadcast_in_dim | solution.py:344
  3.8 48.1 %fused_layer.1 = bf16[768,256]{1,0:T(8,128)(2,1)} custom-call(bf16[768,256]{1,0:T(8,128)(2,1)} %tokens.1, f32[1,1024]{1,0:T(1,128)} %bitcast.1, bf16[1024,1024]{1,0:T(8,128)(2,1)} %w_ri_h.1, bf16[1024,1024]{1,0:T(8,128)(2,1)} %w_ro_h.1, bf16[1,1024,1024]{2,1,0:T(8,128)(2,1)} %w_ei_h.1, bf16[1,1024,1024]{2,1,0:T(8,128)(2,1)} %w_eo_h.1, ...), custom_call_target="tpu_custom_call" | custom-call | tf_op jit(solution)/shard_map/fused_layer/pallas_call | solution.py:321
  52.0 1.8 %copy.11 = bf16[768,256]{1,0:T(8,128)(2,1)} copy(bf16[768,256]{1,0:T(8,128)(2,1)} %fused_layer.1) | data formatting | bytes 786432
